TPU v7x, 32 devices: a whole 2x2x4 slice. The times are simulated.
32 devices in a mesh: batch: 2 (over y), seq: 4 (over x, core), mp: 4 (over z).
Axes of the slice: x: 2, y: 2, z: 4, core: 2. Of those that a mesh axis runs over, the one named last changes fastest.
Arguments:
- tokens: bfloat16 [4096, 2048], P(('batch', 'seq')), may hold values from -6 to 6
- segment_ids: int32 [2, 2048], P('batch'), may hold values from 0 to 3, never falling along the last dimension, each value on 1 to 1024 neighbouring positions
- attn_gain: float32 [2048], replicated, may hold values from 0.5 to 1.5
- w_query: bfloat16 [2048, 2048], P(None, 'mp'), may hold values from -1 to 1
- w_key: bfloat16 [2048, 512], P(None, 'mp'), may hold values from -1 to 1
- w_value: bfloat16 [2048, 512], P(None, 'mp'), may hold values from -0.125 to 0.125
- w_output: bfloat16 [2048, 2048], P('mp'), may hold values from -1 to 1
- mlp_gain: float32 [2048], replicated, may hold values from 0.5 to 1.5
- w_gate: bfloat16 [2048, 8192], P(None, 'mp'), may hold values from -0.125 to 0.125
- w_up: bfloat16 [2048, 8192], P(None, 'mp'), may hold values from -0.125 to 0.125
- w_down: bfloat16 [8192, 2048], P('mp'), may hold values from -0.0625 to 0.0625
- cotangent: bfloat16 [4096, 2048], P(('batch', 'seq')), may hold values from -6 to 6
Outputs:
- output: bfloat16 [4096, 2048], P(('batch', 'seq'))
- grad_tokens: bfloat16 [4096, 2048], P(('batch', 'seq'))
- grad_attn_gain: float32 [2048], P(('batch', 'seq'))
- grad_query: float32 [2048, 2048], P(('batch', 'seq'), 'mp')
- grad_key: float32 [2048, 512], P(('batch', 'seq'), 'mp')
- grad_value: float32 [2048, 512], P(('batch', 'seq'), 'mp')
- grad_output: float32 [2048, 2048], P('mp', ('batch', 'seq'))
- grad_mlp_gain: float32 [2048], P(('batch', 'seq'))
- grad_gate: float32 [2048, 8192], P(('batch', 'seq'), 'mp')
- grad_up: float32 [2048, 8192], P(('batch', 'seq'), 'mp')
- grad_down: float32 [8192, 2048], P('mp', ('batch', 'seq'))
Inputs may be any that keep to these rules, and one draw needn't show every extreme that they name: `segment_ids`: within a row the ids never fall; a document (a run of one id) has 1 to 1024 tokens, and some document has exactly 1024.
All inputs are finite; a program needn't handle non-finite values.
Results may differ from a plain program's by a relative error of at most 0.025.
Values may be sent and summed in bfloat16 or wider, within the bound.
A program may use at most 256 MiB of HBM per device.

v0:
```python
import math
import jax
import jax.numpy as jnp
from jax import lax
from jax.sharding import PartitionSpec as P

HS = 64
rope_base = 500000.0
epsilon = 1e-05
masked_score = -1e30


def tables(seq_ids):
    positions = jnp.arange(seq_ids.shape[0], dtype=jnp.int32)
    before = jnp.concatenate([seq_ids[:1] - 1, seq_ids[:-1]])
    doc_start = lax.cummax(jnp.where(seq_ids != before, positions, 0), axis=0)
    doc_place = (positions - doc_start).astype(jnp.float32)
    half_width = HS // 2
    frequency = jnp.exp(
        jnp.arange(half_width, dtype=jnp.float32) * (-2.0 * math.log(rope_base) / HS)
    )
    angles = doc_place[:, None] * frequency[None, :]
    angles = jnp.concatenate([angles, angles], axis=1)
    return (jnp.cos(angles), jnp.sin(angles))


def rotate_half(values):
    half_width = values.shape[-1] // 2
    return jnp.concatenate([-values[..., half_width:], values[..., :half_width]], axis=-1)


def rope_apply(values, cos_table, sin_table):
    return values * cos_table + rotate_half(values) * sin_table


def rope_back(gradient, cos_table, sin_table):
    return gradient * cos_table - rotate_half(gradient * sin_table)


def product(left_side, right_side):
    return jnp.dot(left_side, right_side, preferred_element_type=jnp.float32)


def score_block(query_block, key_all, segments, first_row):
    score_scale = HS ** (-0.5)
    scores = (
        jnp.einsum("qgrd,kgd->grqk", query_block, key_all, preferred_element_type=jnp.float32)
        * score_scale
    )
    row_count = query_block.shape[0]
    row_index = first_row + jnp.arange(row_count, dtype=jnp.int32)
    key_index = jnp.arange(key_all.shape[0], dtype=jnp.int32)
    row_segment = lax.dynamic_slice_in_dim(segments, first_row, row_count, 0)
    allowed = (row_segment[:, None] == segments[None, :]) & (
        key_index[None, :] <= row_index[:, None]
    )
    return (scores, allowed)


def attend_forward(queries, key_all, value_all, segments, first_row):
    total_rows = queries.shape[0]
    block_rows = min(512, total_rows)

    def one_block(block_start):
        query_block = lax.dynamic_slice_in_dim(queries, block_start, block_rows, 0)
        scores, allowed = score_block(query_block, key_all, segments, first_row + block_start)
        scores = jnp.where(allowed[None, None], scores, masked_score)
        row_max = jnp.max(scores, axis=-1, keepdims=True)
        powers = jnp.exp(scores - row_max)
        totals = jnp.sum(powers, axis=-1, keepdims=True)
        shares = (powers / totals).astype(jnp.bfloat16)
        mixed_out = jnp.einsum(
            "grqk,kgd->qgrd", shares, value_all, preferred_element_type=jnp.float32
        )
        return (mixed_out.astype(jnp.bfloat16), (row_max + jnp.log(totals))[..., 0])

    starts = jnp.arange(total_rows // block_rows, dtype=jnp.int32) * block_rows
    mixed_out, log_total = lax.map(one_block, starts)
    return (mixed_out.reshape(queries.shape), log_total)


def attend_backward(
    queries, key_all, value_all, grad_mixed, log_total, segments, first_row, group_size
):
    total_rows, group_count, head_count, head_width = queries.shape
    copies = head_count // group_size
    block_rows = min(512, total_rows)
    seq_length = key_all.shape[0]
    score_scale = HS ** (-0.5)

    def one_block(carried, inputs):
        grad_key_acc, grad_value_acc = carried
        block_start, log_block = inputs
        query_block = lax.dynamic_slice_in_dim(queries, block_start, block_rows, 0)
        grad_block = lax.dynamic_slice_in_dim(grad_mixed, block_start, block_rows, 0)
        scores, allowed = score_block(query_block, key_all, segments, first_row + block_start)
        shares = jnp.where(allowed[None, None], jnp.exp(scores - log_block[..., None]), 0.0)
        shares_low = shares.astype(jnp.bfloat16)
        grad_split = grad_block.reshape(block_rows, group_count, copies, group_size, head_width)
        grad_value_acc = grad_value_acc + jnp.einsum(
            "gcjqk,qgcjd->kgcd",
            shares_low.reshape(group_count, copies, group_size, block_rows, seq_length),
            grad_split,
            preferred_element_type=jnp.float32,
        )
        grad_shares = jnp.einsum(
            "qgrd,kgd->grqk", grad_block, value_all, preferred_element_type=jnp.float32
        )
        grad_scores = shares * (grad_shares - jnp.sum(shares * grad_shares, axis=-1, keepdims=True))
        scores_low = grad_scores.astype(jnp.bfloat16)
        grad_query = (
            jnp.einsum("grqk,kgd->qgrd", scores_low, key_all, preferred_element_type=jnp.float32)
            * score_scale
        )
        grad_key_acc = (
            grad_key_acc
            + jnp.einsum(
                "gcjqk,qgcjd->kgcd",
                scores_low.reshape(group_count, copies, group_size, block_rows, seq_length),
                query_block.reshape(block_rows, group_count, copies, group_size, head_width),
                preferred_element_type=jnp.float32,
            )
            * score_scale
        )
        return ((grad_key_acc, grad_value_acc), grad_query)

    zero_state = jnp.zeros((seq_length, group_count, copies, head_width), jnp.float32)
    starts = jnp.arange(total_rows // block_rows, dtype=jnp.int32) * block_rows
    (grad_key_acc, grad_value_acc), grad_query = lax.scan(
        one_block, (zero_state, zero_state), (starts, log_total)
    )
    return (grad_query.reshape(queries.shape), grad_key_acc, grad_value_acc)


def local(
    tokens,
    segment_ids,
    attn_gain,
    w_query,
    w_key,
    w_value,
    w_output,
    mlp_gain,
    w_gate,
    w_up,
    w_down,
    cotangent,
):
    row_count = tokens.shape[0]
    seq_count = lax.axis_size("seq")
    seq_index = lax.axis_index("seq")
    segments = segment_ids[0]
    seq_length = segments.shape[0]
    first_row = seq_index * row_count
    cos_table, sin_table = tables(segments)
    cos_local = lax.dynamic_slice_in_dim(cos_table, first_row, row_count, 0)[:, None, :]
    sin_local = lax.dynamic_slice_in_dim(sin_table, first_row, row_count, 0)[:, None, :]
    heads_local = w_query.shape[1] // HS
    kv_local = w_key.shape[1] // HS
    group_size = heads_local // kv_local
    per_device = heads_local // seq_count
    copies = group_size // per_device
    inputs_wide = tokens.astype(jnp.float32)
    scale_one = lax.rsqrt(jnp.mean(inputs_wide * inputs_wide, axis=-1, keepdims=True) + epsilon)
    normed = (inputs_wide * scale_one * attn_gain).astype(jnp.bfloat16)
    query_rot = rope_apply(
        product(normed, w_query).reshape(row_count, heads_local, HS), cos_local, sin_local
    ).astype(jnp.bfloat16)
    key_rot = rope_apply(
        product(normed, w_key).reshape(row_count, kv_local, HS), cos_local, sin_local
    ).astype(jnp.bfloat16)
    value_low = product(normed, w_value).reshape(row_count, kv_local, HS).astype(jnp.bfloat16)
    key_slots = jnp.repeat(key_rot, copies, axis=1)
    value_slots = jnp.repeat(value_low, copies, axis=1)
    pair_slots = jnp.concatenate([key_slots, value_slots], axis=2)
    query_slots = query_rot.reshape(row_count, seq_count, per_device * HS)
    query_heads, pair_heads = (
        lax.all_to_all(query_slots, "seq", split_axis=1, concat_axis=0, tiled=True),
        lax.all_to_all(pair_slots, "seq", split_axis=1, concat_axis=0, tiled=True),
    )
    query_heads = query_heads.reshape(seq_length, 1, per_device, HS)
    key_heads = pair_heads[:, :, :HS]
    value_heads = pair_heads[:, :, HS:]
    mixed_heads, log_total = attend_forward(query_heads, key_heads, value_heads, segments, 0)
    mixed_back = lax.all_to_all(
        mixed_heads.reshape(seq_length, 1, per_device * HS),
        "seq",
        split_axis=0,
        concat_axis=1,
        tiled=True,
    )
    mixed_out = mixed_back.reshape(row_count, heads_local * HS)
    branch = lax.psum(product(mixed_out, w_output).astype(jnp.bfloat16), "mp").astype(jnp.float32)
    middle = inputs_wide + branch
    scale_two = lax.rsqrt(jnp.mean(middle * middle, axis=-1, keepdims=True) + epsilon)
    normed_two = (middle * scale_two * mlp_gain).astype(jnp.bfloat16)
    gate_pre = product(normed_two, w_gate)
    up_pre = product(normed_two, w_up)
    sigmoid_gate = jax.nn.sigmoid(gate_pre)
    swish_gate = gate_pre * sigmoid_gate
    active = (swish_gate * up_pre).astype(jnp.bfloat16)
    mlp_out = lax.psum(product(active, w_down).astype(jnp.bfloat16), "mp").astype(jnp.float32)
    output = (middle + mlp_out).astype(jnp.bfloat16)
    grad_down = jnp.einsum("tf,td->fd", active, cotangent, preferred_element_type=jnp.float32)
    grad_active = jnp.einsum("td,fd->tf", cotangent, w_down, preferred_element_type=jnp.float32)
    grad_gate_low = (
        grad_active * up_pre * sigmoid_gate * (1.0 + gate_pre * (1.0 - sigmoid_gate))
    ).astype(jnp.bfloat16)
    grad_up_low = (grad_active * swish_gate).astype(jnp.bfloat16)
    grad_gate_w = jnp.einsum(
        "td,tf->df", normed_two, grad_gate_low, preferred_element_type=jnp.float32
    )
    grad_up_w = jnp.einsum("td,tf->df", normed_two, grad_up_low, preferred_element_type=jnp.float32)
    grad_normed_two = lax.psum(
        (
            jnp.einsum("tf,df->td", grad_gate_low, w_gate, preferred_element_type=jnp.float32)
            + jnp.einsum("tf,df->td", grad_up_low, w_up, preferred_element_type=jnp.float32)
        ).astype(jnp.bfloat16),
        "mp",
    ).astype(jnp.float32)
    scaled_two = grad_normed_two * mlp_gain
    grad_middle = (
        cotangent.astype(jnp.float32)
        + scale_two * scaled_two
        - middle
        * (scale_two * scale_two * scale_two)
        * jnp.mean(middle * scaled_two, axis=-1, keepdims=True)
    )
    grad_mlp_gain = jnp.sum(grad_normed_two * middle * scale_two, axis=0)
    grad_branch = grad_middle.astype(jnp.bfloat16)
    grad_output_w = jnp.einsum(
        "tc,td->cd", mixed_out, grad_branch, preferred_element_type=jnp.float32
    )
    grad_mixed = jnp.einsum(
        "td,cd->tc", grad_branch, w_output, preferred_element_type=jnp.float32
    ).astype(jnp.bfloat16)
    grad_heads = lax.all_to_all(
        grad_mixed.reshape(row_count, seq_count, per_device * HS),
        "seq",
        split_axis=1,
        concat_axis=0,
        tiled=True,
    )
    grad_heads = grad_heads.reshape(seq_length, 1, per_device, HS)
    grad_query, grad_key_copy, grad_value_copy = attend_backward(
        query_heads, key_heads, value_heads, grad_heads, log_total, segments, 0, per_device
    )
    cos_wide = cos_table[:, None, None, :]
    sin_wide = sin_table[:, None, None, :]
    grad_query_low = rope_back(grad_query, cos_wide, sin_wide).astype(jnp.bfloat16)
    grad_key_low = rope_back(grad_key_copy, cos_wide, sin_wide).astype(jnp.bfloat16)
    grad_pair = jnp.concatenate(
        [grad_key_low, grad_value_copy.astype(jnp.bfloat16)], axis=3
    ).reshape(seq_length, 1, 2 * HS)
    grad_query_tok, grad_pair_tok = (
        lax.all_to_all(
            grad_query_low.reshape(seq_length, 1, per_device * HS),
            "seq",
            split_axis=0,
            concat_axis=1,
            tiled=True,
        ),
        lax.all_to_all(grad_pair, "seq", split_axis=0, concat_axis=1, tiled=True),
    )
    grad_query_pre = grad_query_tok.reshape(row_count, heads_local * HS)
    pair_summed = jnp.sum(
        grad_pair_tok.astype(jnp.float32).reshape(row_count, kv_local, copies, 2 * HS), axis=2
    )
    grad_key_pre = pair_summed[:, :, :HS].reshape(row_count, kv_local * HS).astype(jnp.bfloat16)
    grad_value_pre = pair_summed[:, :, HS:].reshape(row_count, kv_local * HS).astype(jnp.bfloat16)
    grad_query_w = jnp.einsum(
        "td,tc->dc", normed, grad_query_pre, preferred_element_type=jnp.float32
    )
    grad_key_w = jnp.einsum("td,tc->dc", normed, grad_key_pre, preferred_element_type=jnp.float32)
    grad_value_w = jnp.einsum(
        "td,tc->dc", normed, grad_value_pre, preferred_element_type=jnp.float32
    )
    grad_normed = lax.psum(
        (
            jnp.einsum("tc,dc->td", grad_query_pre, w_query, preferred_element_type=jnp.float32)
            + jnp.einsum("tc,dc->td", grad_key_pre, w_key, preferred_element_type=jnp.float32)
            + jnp.einsum("tc,dc->td", grad_value_pre, w_value, preferred_element_type=jnp.float32)
        ).astype(jnp.bfloat16),
        "mp",
    ).astype(jnp.float32)
    scaled_one = grad_normed * attn_gain
    grad_inputs = (
        grad_middle
        + scale_one * scaled_one
        - inputs_wide
        * (scale_one * scale_one * scale_one)
        * jnp.mean(inputs_wide * scaled_one, axis=-1, keepdims=True)
    )
    grad_attn_gain = jnp.sum(grad_normed * inputs_wide * scale_one, axis=0)
    grad_tokens = grad_inputs.astype(jnp.bfloat16)
    summed = (
        lax.psum_scatter(
            grad_attn_gain.astype(jnp.bfloat16), ("batch", "seq"), scatter_dimension=0, tiled=True
        ).astype(jnp.float32),
        lax.psum_scatter(
            grad_query_w.astype(jnp.bfloat16), ("batch", "seq"), scatter_dimension=0, tiled=True
        ).astype(jnp.float32),
        lax.psum_scatter(
            grad_key_w.astype(jnp.bfloat16), ("batch", "seq"), scatter_dimension=0, tiled=True
        ).astype(jnp.float32),
        lax.psum_scatter(
            grad_value_w.astype(jnp.bfloat16), ("batch", "seq"), scatter_dimension=0, tiled=True
        ).astype(jnp.float32),
        lax.psum_scatter(
            grad_output_w.astype(jnp.bfloat16), ("batch", "seq"), scatter_dimension=1, tiled=True
        ).astype(jnp.float32),
        lax.psum_scatter(
            grad_mlp_gain.astype(jnp.bfloat16), ("batch", "seq"), scatter_dimension=0, tiled=True
        ).astype(jnp.float32),
        lax.psum_scatter(
            grad_gate_w.astype(jnp.bfloat16), ("batch", "seq"), scatter_dimension=0, tiled=True
        ).astype(jnp.float32),
        lax.psum_scatter(
            grad_up_w.astype(jnp.bfloat16), ("batch", "seq"), scatter_dimension=0, tiled=True
        ).astype(jnp.float32),
        lax.psum_scatter(
            grad_down.astype(jnp.bfloat16), ("batch", "seq"), scatter_dimension=1, tiled=True
        ).astype(jnp.float32),
    )
    return (
        output,
        grad_tokens,
        summed[0],
        summed[1],
        summed[2],
        summed[3],
        summed[4],
        summed[5],
        summed[6],
        summed[7],
        summed[8],
    )


def solution(mesh):
    in_specs = (
        P(("batch", "seq"), None),
        P("batch", None),
        P(),
        P(None, "mp"),
        P(None, "mp"),
        P(None, "mp"),
        P("mp", None),
        P(),
        P(None, "mp"),
        P(None, "mp"),
        P("mp", None),
        P(("batch", "seq"), None),
    )
    out_specs = (
        P(("batch", "seq"), None),
        P(("batch", "seq"), None),
        P(("batch", "seq")),
        P(("batch", "seq"), "mp"),
        P(("batch", "seq"), "mp"),
        P(("batch", "seq"), "mp"),
        P("mp", ("batch", "seq")),
        P(("batch", "seq")),
        P(("batch", "seq"), "mp"),
        P(("batch", "seq"), "mp"),
        P("mp", ("batch", "seq")),
    )
    return jax.shard_map(local, mesh=mesh, in_specs=in_specs, out_specs=out_specs, check_vma=False)
```

profile of v0, /device:TPU:0, one launch (start us, length us, event | category | flops | bytes accessed | tf_op | source)
XLA Modules:
  0.0 1099.2 jit_solution(13125591783962021573)
XLA Ops:
  54.6 49.3 %while.27 = (s32[]{:T(128)}, bf16[4,512,1,2,64]{1,4,3,2,0:T(8,128)(2,1)}, f32[4,1,2,512]{3,2,1,0:T(2,128)S(1)}, s32[4]{0:T(128)S(1)}, s32[2048]{0:T(1024)S(1)}, ...) while((s32[]{:T(128)}, ...), condition=%wide.region_6.7_spmd, body=%wide.region_3.6_spmd.sunk | while | flops 565247488 | bytes 30198452 | solution.py:78
  113.0 13.4 %reduce.6 = bf16[2048,128]{1,0:T(8,128)(2,1)} reduce(bf16[2048,1,128]{2,1,0:T(2,128)(2,1)} %reshape.582, bf16[]{:T(256)} %broadcast.317), dimensions={1}, to_apply=%reshape.582.reduce_sub_computation | reduce | bytes 1048578 | tf_op jit(solution)/shard_map/reshape;reshape | solution.py:186
  128.3 13.4 %all_to_all.87 = bf16[4,2,32768]{2,1,0:T(2,128)(2,1)} all-to-all(bf16[4,2,32768]{2,1,0:T(2,128)(2,1)} %reshape.586), channel_id=1, replica_groups=mesh['batch'=2,'seq'=4,'mp'=4] {'seq'}, dimensions={0} | all-to-all | bytes 1048576 | tf_op jit(solution)/shard_map/all_to_all | solution.py:185
  153.0 87.3 %all-reduce.8.cloned.1.call-done = bf16[512,2048]{1,0:T(8,128)(2,1)} async-done(((bf16[512,2048]{1,0:T(8,128)(2,1)}), bf16[512,2048]{1,0:T(8,128)(2,1)}) %all-reduce.8.cloned.1.call-update) | async-done | bytes 2097168 | tf_op jit(solution)/shard_map/psum | solution.py:193
  244.9 7.7 fusion.109
  258.8 11.9 %multiply_convert_fusion = (bf16[512,2048]{1,0:T(8,128)(2,1)}, bf16[512,2048]{1,0:T(8,128)(2,1)}, bf16[512,2048]{1,0:T(8,128)(2,1)}) fusion(f32[512,2048]{1,0:T(8,128)S(1)} %fusion.109, f32[512,2048]{1,0:T(8,128)} %fusion.110, bf16[512,2048]{1,0:T(8,128)(2,1)S(1)} %copy-done.21, bf16[2048,2048]{1,0:T(8,128)(2,1)} %param.26), kind=kOutput, calls=%fused_computation.98 | convolution fusion | flops 4310695936 | bytes 25165824 | tf_op jit(solution)/shard_map/td,fd->tf/dot_general | solution.py:205
  270.7 7.8 fusion.111
  278.5 9.6 add_convert_fusion.1
  288.1 85.4 %all-reduce.10.cloned.1.call-done = bf16[512,2048]{1,0:T(8,128)(2,1)} async-done(((bf16[512,2048]{1,0:T(8,128)(2,1)}), bf16[512,2048]{1,0:T(8,128)(2,1)}) %all-reduce.10.cloned.1.call-update) | async-done | bytes 2097168 | tf_op jit(solution)/shard_map/psum | solution.py:214
  389.3 8.7 all-to-all-done.3
  398.8 124.7 %while.28 = (s32[]{:T(128)}, f32[2048,1,1,64]{0,3,2,1:T(8,128)S(1)}, f32[2048,1,1,64]{0,3,2,1:T(8,128)}, f32[4,512,1,2,64]{1,0,4,3,2:T(4,128)}, s32[4]{0:T(128)S...) while((s32[]{:T(128)}, ...), condition=%wide.region_14.15_spmd.clone, body=%wide.region_12.14_spmd.clone.sunk | while | flops 1377500672 | bytes 126400856 | solution.py:129
  414.0 6.1 dynamic_update_slice.20
  423.3 6.6 fusion.190
  445.2 6.1 dynamic_update_slice.20
  454.5 6.6 fusion.190
  476.4 6.1 dynamic_update_slice.20
  485.7 6.6 fusion.190
  516.9 6.6 fusion.190
  530.1 12.0 %all_to_all.88 = bf16[4,2,32768]{2,1,0:T(2,128)(2,1)} all-to-all(bf16[4,2,32768]{2,1,0:T(2,128)(2,1)S(1)} %reshape.590), channel_id=1, replica_groups=mesh['batch'=2,'seq'=4,'mp'=4] {'seq'}, dimensions={0} | all-to-all | bytes 1048576 | tf_op jit(solution)/shard_map/all_to_all | solution.py:263
  564.9 11.9 %all_to_all.89 = bf16[4,2,32768]{2,1,0:T(2,128)(2,1)} all-to-all(bf16[4,2,32768]{2,1,0:T(2,128)(2,1)S(1)} %reshape.588), channel_id=1, replica_groups=mesh['batch'=2,'seq'=4,'mp'=4] {'seq'}, dimensions={0} | all-to-all | bytes 1048576 | tf_op jit(solution)/shard_map/all_to_all | solution.py:256
  584.2 9.9 convolution_convert_fusion.5
  599.2 10.0 convolution_convert_fusion.2
  609.5 10.0 convolution_convert_fusion.1
  619.6 10.0 convolution_convert_fusion
  634.5 29.0 %reduce-scatter.14.cloned.1.call-done = bf16[512,256]{1,0:T(8,128)(2,1)} async-done(((bf16[512,2048]{1,0:T(8,128)(2,1)}), bf16[512,256]{1,0:T(8,128)(2,1)}) %reduce-scatter.14.cloned.1.call-update) | async-done | bytes 262160 | tf_op jit(solution)/shard_map/reduce_scatter | solution.py:309
  665.4 42.5 %reduce-scatter.8.cloned.1.call-done = bf16[256,512]{1,0:T(8,128)(2,1)} async-done(((bf16[2048,512]{1,0:T(8,128)(2,1)}), bf16[256,512]{1,0:T(8,128)(2,1)}) %reduce-scatter.8.cloned.1.call-update) | async-done | bytes 262160 | tf_op jit(solution)/shard_map/reduce_scatter | solution.py:300
  709.6 156.2 %all-reduce.12.cloned.1.call-done = (bf16[512,2048]{1,0:T(8,128)(2,1)}, bf16[512,2048]{1,0:T(8,128)(2,1)}) async-done(((bf16[512,2048]{1,0:T(8,128)(2,1)}, bf16[512,2048]{1,0:T(8,128)(2,1)}), (bf16[512,2048]{1,0:T(8,128)(2,1)}, bf16[512,2048]{1,0:T(8,128)(2,1)})) %all-reduce.12.cloned.1.call-update) | async-done | bytes 4194320 | tf_op jit(solution)/shard_map/psum | solution.py:202
  869.0 13.7 %all-reduce.2 = (bf16[2048]{0:T(1024)(128)(2,1)S(1)}, bf16[2048]{0:T(1024)(128)(2,1)S(1)}) all-reduce(bf16[2048]{0:T(1024)(128)(2,1)S(1)} %get-tuple-element.211, bf16[2048]{0:T(1024)(128)(2,1)S(1)} %copy-done.32), channel_id=2, replica_groups=mesh['batch'=2,'seq'=4,'mp'=4] {'batch','seq'}, use_global_device_ids=true, to_apply=%region_19.20.clone | all-reduce | flops 4096 | bytes 16384
  884.0 7.3 fusion.68
  891.3 48.5 %reduce-scatter.16.cloned.1.call-done = bf16[256,2048]{1,0:T(8,128)(2,1)} async-done(((bf16[2048,2048]{1,0:T(8,128)(2,1)}), bf16[256,2048]{1,0:T(8,128)(2,1)}) %reduce-scatter.16.cloned.1.call-update) | async-done | bytes 1048592 | tf_op jit(solution)/shard_map/reduce_scatter | solution.py:315
  942.6 72.2 %reduce-scatter.18.cloned.1.call-done = bf16[256,2048]{1,0:T(8,128)(2,1)} async-done(((bf16[2048,2048]{1,0:T(8,128)(2,1)}), bf16[256,2048]{1,0:T(8,128)(2,1)}) %reduce-scatter.18.cloned.1.call-update) | async-done | bytes 1048592 | tf_op jit(solution)/shard_map/reduce_scatter | solution.py:318
  1017.6 71.8 %reduce-scatter.20.cloned.1.call-done = bf16[2048,256]{1,0:T(8,128)(2,1)} async-done(((bf16[2048,2048]{1,0:T(8,128)(2,1)}), bf16[2048,256]{1,0:T(8,128)(2,1)}) %reduce-scatter.20.cloned.1.call-update) | async-done | bytes 1048592 | tf_op jit(solution)/shard_map/reduce_scatter | solution.py:321
  (306 shorter events, 271.4 us)
Async XLA Ops:
  7.2 142.1 %copy-start = (bf16[512,2048]{1,0:T(8,128)(2,1)S(1)}, bf16[512,2048]{1,0:T(8,128)(2,1)}, u32[]{:S(2)}) copy-start(bf16[512,2048]{1,0:T(8,128)(2,1)} %param.22) | copy-start | bytes 6291460
  10.6 9.7 copy-start.4
  10.6 9.7 copy-start.25
  10.6 9.7 copy-start.28
  13.3 8.7 copy-start.15
  13.3 8.7 copy-start.17
  16.4 12.7 %copy-start.30 = (f32[512]{0:T(512)}, f32[512]{0:T(512)S(1)}, u32[]{:S(2)}) copy-start(f32[512]{0:T(512)S(1)} %get-tuple-element.285) | copy-start | bytes 6148
  24.8 13.1 %all-to-all-start.1 = ((bf16[512,4,128]{0,2,1:T(8,128)(2,1)}), bf16[512,4,128]{0,2,1:T(8,128)(2,1)S(1)}, u32[]{:S(2)}, u32[]{:S(2)}) async-start(bf16[512,4,128]{0,2,1:T(8,128)(2,1)} %pad_maximum_fusion.2), calls=%async_computation.1 | async-start | bytes 1048576 | tf_op jit(solution)/shard_map/all_to_all | solution.py:179
  34.2 20.4 %copy-start.22 = (s32[1,2048]{1,0:T(1,128)S(1)}, s32[1,2048]{1,0:T(1,128)}, u32[]{:S(2)}) copy-start(s32[1,2048]{1,0:T(1,128)} %param.17) | copy-start | bytes 24580
  37.9 13.0 %all-to-all-start = ((bf16[512,4,128]{0,2,1:T(8,128)(2,1)}), bf16[512,4,128]{0,2,1:T(8,128)(2,1)}, u32[]{:S(2)}, u32[]{:S(2)}) async-start(bf16[512,4,128]{0,2,1:T(8,128)(2,1)} %fusion.83), calls=%async_computation | async-start | bytes 1048576 | tf_op jit(solution)/shard_map/all_to_all | solution.py:178
  42.1 198.2 %all-reduce.8.cloned.1.call-start = ((), (), s32[]{:S(2)}) async-start(), calls=%async_computation.13 | async-start | bytes 4194304 | tf_op jit(solution)/shard_map/psum | solution.py:193
  152.9 90.5 %copy-start.27 = (f32[2048]{0:T(1024)S(1)}, f32[2048]{0:T(1024)}, u32[]{:S(2)}) copy-start(f32[2048]{0:T(1024)} %param.23) | copy-start | bytes 24580
  153.0 220.5 %all-reduce.10.cloned.1.call-start = ((), (), s32[]{:S(2)}) async-start(), calls=%async_computation.14 | async-start | bytes 4194304 | tf_op jit(solution)/shard_map/psum | solution.py:214
  243.8 8.9 slice-start
  244.9 7.8 slice-start.1
  385.8 12.3 %all-to-all-start.3 = ((bf16[512,4,128]{0,2,1:T(8,128)(2,1)}), bf16[512,4,128]{0,2,1:T(8,128)(2,1)S(1)}, u32[]{:S(2)}, u32[]{:S(2)}) async-start(bf16[512,4,128]{0,2,1:T(8,128)(2,1)} %bitcast.384), calls=%async_computation.3 | async-start | bytes 1048576 | tf_op jit(solution)/shard_map/all_to_all | solution.py:237
  389.3 242.3 %reduce-scatter.10.cloned.1.call-start = ((), (), s32[]{:S(2)}) async-start(), calls=%async_computation.16 | async-start | bytes 589824 | tf_op jit(solution)/shard_map/reduce_scatter | solution.py:303
  398.8 124.7 %copy-start.18 = (f32[2048,1,1,32]{0,3,2,1:T(8,128)S(1)}, f32[2048,1,1,32]{0,3,2,1:T(8,128)}, u32[]{:S(2)}) copy-start(f32[2048,1,1,32]{0,3,2,1:T(8,128)} %get-tuple-element.282) | copy-start | bytes 786436
  529.6 17.1 %copy-start.7 = (bf16[512,2048]{1,0:T(8,128)(2,1)S(1)}, bf16[512,2048]{1,0:T(8,128)(2,1)}, u32[]{:S(2)}) copy-start(bf16[512,2048]{1,0:T(8,128)(2,1)} %param.16) | copy-start | bytes 6291460
  529.7 17.1 %copy-start.29 = (f32[2048]{0:T(1024)S(1)}, f32[2048]{0:T(1024)}, u32[]{:S(2)}) copy-start(f32[2048]{0:T(1024)} %param.18) | copy-start | bytes 24580
  529.7 17.0 %copy-start.31 = (f32[512]{0:T(512)S(1)}, f32[512]{0:T(512)}, u32[]{:S(2)}) copy-start(f32[512]{0:T(512)} %copy-done.30) | copy-start | bytes 6148
  548.6 84.4 %reduce-scatter.12.cloned.1.call-start = ((), (), s32[]{:S(2)}) async-start(), calls=%async_computation.17 | async-start | bytes 589824 | tf_op jit(solution)/shard_map/reduce_scatter | solution.py:306
  550.7 112.9 %reduce-scatter.14.cloned.1.call-start = ((), (), s32[]{:S(2)}) async-start(), calls=%async_computation.18 | async-start | bytes 2359296 | tf_op jit(solution)/shard_map/reduce_scatter | solution.py:309
  555.9 152.0 %reduce-scatter.8.cloned.1.call-start = ((), (), s32[]{:S(2)}) async-start(), calls=%async_computation.15 | async-start | bytes 2359296 | tf_op jit(solution)/shard_map/reduce_scatter | solution.py:300
  583.9 281.9 %all-reduce.12.cloned.1.call-start = ((), (), s32[]{:S(2)}) async-start(), calls=%async_computation.22 | async-start | bytes 8388608 | tf_op jit(solution)/shard_map/psum | solution.py:202
  584.2 9.9 copy-start.24
  599.1 340.7 %reduce-scatter.16.cloned.1.call-start = ((), (), s32[]{:S(2)}) async-start(), calls=%async_computation.19 | async-start | bytes 9437184 | tf_op jit(solution)/shard_map/reduce_scatter | solution.py:315
  609.2 405.6 %reduce-scatter.18.cloned.1.call-start = ((), (), s32[]{:S(2)}) async-start(), calls=%async_computation.20 | async-start | bytes 9437184 | tf_op jit(solution)/shard_map/reduce_scatter | solution.py:318
  619.5 469.9 %reduce-scatter.20.cloned.1.call-start = ((), (), s32[]{:S(2)}) async-start(), calls=%async_computation.21 | async-start | bytes 9437184 | tf_op jit(solution)/shard_map/reduce_scatter | solution.py:321
  629.6 239.4 %copy-start.32 = (bf16[2048]{0:T(1024)(128)(2,1)S(1)}, bf16[2048]{0:T(1024)(128)(2,1)}, u32[]{:S(2)}) copy-start(bf16[2048]{0:T(1024)(128)(2,1)} %get-tuple-element.209) | copy-start | bytes 12292
  629.6 254.4 %copy-start.33 = (f32[512]{0:T(512)S(1)}, f32[512]{0:T(512)}, u32[]{:S(2)}) copy-start(f32[512]{0:T(512)} %get-tuple-element.284) | copy-start | bytes 6148
  884.0 208.1 %copy-start.1 = (bf16[512,2048]{1,0:T(8,128)(2,1)S(1)}, bf16[512,2048]{1,0:T(8,128)(2,1)}, u32[]{:S(2)}) copy-start(bf16[512,2048]{1,0:T(8,128)(2,1)} %param.22) | copy-start | bytes 6291460
  (31 other events, 128.1 us)
Sparse Core Ops, SparseCore 0:
  153.1 87.1 all-reduce.7
  288.2 85.1 all-reduce.9
  548.7 33.4 reduce-scatter.9
  585.2 34.0 reduce-scatter.11
  622.4 41.0 reduce-scatter.13
  666.7 41.0 reduce-scatter.7
  710.8 154.9 all-reduce.11
  869.3 70.4 reduce-scatter.15
  943.3 71.4 reduce-scatter.17
  1018.1 71.2 reduce-scatter.19
where the time goes:
time: 1110 us; the launch traced here: 1100 us
  waiting for transfers between devices  612 us (55%)
  matrix products  196 us (18%)
  other arithmetic  110 us (10%)
  local copies, waits for them, and re-layouts  85.5 us (8%)
  blocking collectives  51 us (5%)
  between operations  16.4 us (1%)
  loops' own time  16.2 us (1%)
  starting transfers between devices  12.7 us (1%)
    psum x1, waiting for transfers between devices, local(): lax.psum(product(active, w_down).astype(jnp.bfloat16), 'mp')  156 us
    psum x1, waiting for transfers between devices, local(): lax.psum(product(mixed_out, w_output).astype(jnp.bfloat16), 'mp')  87.3 us
    psum x1, waiting for transfers between devices, local(): lax.psum((jnp.einsum('tf,df->td', grad_gate_low, w_gate, preferred_elemen...  85.4 us
    reduce_scatter x1, waiting for transfers between devices, local(): lax.psum_scatter(grad_up_w.astype(jnp.bfloat16), ('batch', 'seq'), scatte...  72.2 us
    reduce_scatter x1, waiting for transfers between devices, local(): lax.psum_scatter(grad_down.astype(jnp.bfloat16), ('batch', 'seq'), scatte...  71.8 us
    reduce_scatter x1, waiting for transfers between devices, local(): lax.psum_scatter(grad_gate_w.astype(jnp.bfloat16), ('batch', 'seq'), scat...  48.5 us
    reduce_scatter x1, waiting for transfers between devices, local(): lax.psum_scatter(grad_query_w.astype(jnp.bfloat16), ('batch', 'seq'), sca...  42.5 us
    dot_general x7, matrix products, product(): return jnp.dot(left_side, right_side, preferred_element_type=jnp.float32)  35.1 us
  transfers between devices with their start and end apart: 13, of which 11 were waited for; matrix products, arithmetic and copies ran while one was open for 9% of the time, Pallas kernels for 0%

commit v1 on v0

--- a/solution.py
+++ b/solution.py
@@ -3,6 +3,7 @@
 import jax.numpy as jnp
 from jax import lax
 from jax.sharding import PartitionSpec as P
+from jax.lax import all_gather
 
 HS = 64
 rope_base = 500000.0
@@ -211,12 +212,15 @@
         "td,tf->df", normed_two, grad_gate_low, preferred_element_type=jnp.float32
     )
     grad_up_w = jnp.einsum("td,tf->df", normed_two, grad_up_low, preferred_element_type=jnp.float32)
-    grad_normed_two = lax.psum(
-        (
-            jnp.einsum("tf,df->td", grad_gate_low, w_gate, preferred_element_type=jnp.float32)
-            + jnp.einsum("tf,df->td", grad_up_low, w_up, preferred_element_type=jnp.float32)
-        ).astype(jnp.bfloat16),
-        "mp",
+    grad_normed_two = jnp.sum(
+        all_gather(
+            (
+                jnp.einsum("tf,df->td", grad_gate_low, w_gate, preferred_element_type=jnp.float32)
+                + jnp.einsum("tf,df->td", grad_up_low, w_up, preferred_element_type=jnp.float32)
+            ).astype(jnp.bfloat16),
+            axis_name="mp",
+        ),
+        axis=0,
     ).astype(jnp.float32)
     scaled_two = grad_normed_two * mlp_gain
     grad_middle = (

time: 1110 us -> 1030 us (0.928)
  waiting for transfers between devices: 612 us -> 509 us
    all_gather x0 -> x1, waiting for transfers between devices: none -> 128 us  [local(): all_gather((jnp.einsum('tf,df->td', grad_gate_low, w_gate, preferred_elem...]
    psum x1 -> x0, waiting for transfers between devices: 85.4 us -> none  [local(): lax.psum((jnp.einsum('tf,df->td', grad_gate_low, w_gate, preferred_elemen...]
    reduce_scatter x1, waiting for transfers between devices: 72.2 us -> 0.01 us  [local(): lax.psum_scatter(grad_up_w.astype(jnp.bfloat16), ('batch', 'seq'), scatte...]
    reduce_scatter x1, waiting for transfers between devices: 71.8 us -> 0.01 us  [local(): lax.psum_scatter(grad_down.astype(jnp.bfloat16), ('batch', 'seq'), scatte...]
    reduce_scatter x1, waiting for transfers between devices: 48.5 us -> 0.02 us  [local(): lax.psum_scatter(grad_gate_w.astype(jnp.bfloat16), ('batch', 'seq'), scat...]
    reduce_scatter x1, waiting for transfers between devices: 0.01 us -> 35.7 us  [local(): lax.psum_scatter(grad_value_w.astype(jnp.bfloat16), ('batch', 'seq'), sca...]
    reduce_scatter x1, waiting for transfers between devices: 29 us -> 42.9 us  [local(): lax.psum_scatter(grad_output_w.astype(jnp.bfloat16), ('batch', 'seq'), sc...]
  transfers between devices with their start and end apart: 13 -> 13, of which waited for: 11 -> 10; matrix products, arithmetic and copies ran while one was open for 9% -> 23% of each run, Pallas kernels for 0% -> 0%
where the time goes in v1:
time: 1030 us; the launch traced here: 1020 us
  waiting for transfers between devices  509 us (49%)
  matrix products  197 us (19%)
  other arithmetic  118 us (11%)
  local copies, waits for them, and re-layouts  86 us (8%)
  blocking collectives  61.6 us (6%)
  between operations  16.4 us (2%)
  loops' own time  16.2 us (2%)
  starting transfers between devices  13.1 us (1%)
    psum x1, waiting for transfers between devices, local(): lax.psum(product(active, w_down).astype(jnp.bfloat16), 'mp')  156 us
    all_gather x1, waiting for transfers between devices, local(): all_gather((jnp.einsum('tf,df->td', grad_gate_low, w_gate, preferred_elem...  128 us
    psum x1, waiting for transfers between devices, local(): lax.psum(product(mixed_out, w_output).astype(jnp.bfloat16), 'mp')  87.2 us
    reduce_scatter x1, waiting for transfers between devices, local(): lax.psum_scatter(grad_output_w.astype(jnp.bfloat16), ('batch', 'seq'), sc...  42.9 us
    reduce_scatter x1, waiting for transfers between devices, local(): lax.psum_scatter(grad_query_w.astype(jnp.bfloat16), ('batch', 'seq'), sca...  42.6 us
    reduce_scatter x1, waiting for transfers between devices, local(): lax.psum_scatter(grad_value_w.astype(jnp.bfloat16), ('batch', 'seq'), sca...  35.7 us
    dot_general x7, matrix products, product(): return jnp.dot(left_side, right_side, preferred_element_type=jnp.float32)  34.2 us
    dot_general x4, matrix products, one_block(): jnp.einsum('gcjqk,qgcjd->kgcd', shares_low.reshape(group_count, copies, g...  27.7 us
  transfers between devices with their start and end apart: 13, of which 10 were waited for; matrix products, arithmetic and copies ran while one was open for 23% of the time, Pallas kernels for 0%

profile of v1, /device:TPU:0, one launch (start us, length us, event | category | flops | bytes accessed | tf_op | source)
XLA Modules:
  0.0 1017.3 jit_solution(16741404361178364633)
XLA Ops:
  54.6 49.3 %while.27 = (s32[]{:T(128)}, bf16[4,512,1,2,64]{1,4,3,2,0:T(8,128)(2,1)}, f32[4,1,2,512]{3,2,1,0:T(2,128)S(1)}, s32[4]{0:T(128)S(1)}, s32[2048]{0:T(1024)S(1)}, ...) while((s32[]{:T(128)}, ...), condition=%wide.region_6.7_spmd, body=%wide.region_3.6_spmd.sunk | while | flops 565247488 | bytes 30198452 | solution.py:79
  113.1 13.4 %reduce.7 = bf16[2048,128]{1,0:T(8,128)(2,1)} reduce(bf16[2048,1,128]{2,1,0:T(2,128)(2,1)} %reshape.583, bf16[]{:T(256)} %broadcast.317), dimensions={1}, to_apply=%reshape.583.reduce_sub_computation | reduce | bytes 1048578 | tf_op jit(solution)/shard_map/reshape;reshape | solution.py:187
  128.4 13.4 %all_to_all.87 = bf16[4,2,32768]{2,1,0:T(2,128)(2,1)} all-to-all(bf16[4,2,32768]{2,1,0:T(2,128)(2,1)} %reshape.587), channel_id=1, replica_groups=mesh['batch'=2,'seq'=4,'mp'=4] {'seq'}, dimensions={0} | all-to-all | bytes 1048576 | tf_op jit(solution)/shard_map/all_to_all | solution.py:186
  151.4 87.2 %all-reduce.7.cloned.1.call-done = bf16[512,2048]{1,0:T(8,128)(2,1)} async-done(((bf16[512,2048]{1,0:T(8,128)(2,1)}), bf16[512,2048]{1,0:T(8,128)(2,1)}) %all-reduce.7.cloned.1.call-update) | async-done | bytes 2097168 | tf_op jit(solution)/shard_map/psum | solution.py:194
  243.2 7.7 fusion.109
  251.0 6.1 fusion.110
  257.1 11.9 %multiply_convert_fusion = (bf16[512,2048]{1,0:T(8,128)(2,1)}, bf16[512,2048]{1,0:T(8,128)(2,1)}, bf16[512,2048]{1,0:T(8,128)(2,1)}) fusion(f32[512,2048]{1,0:T(8,128)S(1)} %fusion.109, f32[512,2048]{1,0:T(8,128)} %fusion.110, bf16[512,2048]{1,0:T(8,128)(2,1)S(1)} %copy-done.22, bf16[2048,2048]{1,0:T(8,128)(2,1)} %param.26), kind=kOutput, calls=%fused_computation.98 | convolution fusion | flops 4310695936 | bytes 25165824 | tf_op jit(solution)/shard_map/td,fd->tf/dot_general | solution.py:206
  269.1 7.8 fusion.111
  276.8 9.4 add_convert_fusion.1
  286.5 10.6 %convolution_convert_fusion.2 = bf16[2048,2048]{1,0:T(8,128)(2,1)} fusion(bf16[512,2048]{1,0:T(8,128)(2,1)} %copy-done.21, bf16[512,2048]{1,0:T(8,128)(2,1)} %get-tuple-element.264), kind=kOutput, calls=%fused_computation.74 | convolution fusion | flops 4299161600 | bytes 12582912 | tf_op jit(solution)/shard_map/td,tf->df/dot_general | solution.py:211
  297.1 10.4 %convolution_convert_fusion.1 = bf16[2048,2048]{1,0:T(8,128)(2,1)} fusion(bf16[512,2048]{1,0:T(8,128)(2,1)} %copy-done.21, bf16[512,2048]{1,0:T(8,128)(2,1)} %get-tuple-element.263), kind=kOutput, calls=%fused_computation.73 | convolution fusion | flops 4299161600 | bytes 12582912 | tf_op jit(solution)/shard_map/td,tf->df/dot_general | solution.py:214
  307.6 127.5 %all-gather.3.cloned.1.call-done = bf16[2048,2048]{1,0:T(8,128)(2,1)} async-done(((bf16[512,2048]{1,0:T(8,128)(2,1)}), bf16[2048,2048]{1,0:T(8,128)(2,1)}) %all-gather.3.cloned.1.call-update) | async-done | bytes 8388624 | tf_op jit(solution)/shard_map/all_gather | solution.py:216
  435.1 7.2 reduce_sum.95
  460.1 10.1 convolution_convert_fusion
  473.8 126.9 %while.28 = (s32[]{:T(128)}, f32[2048,1,1,64]{0,3,2,1:T(8,128)S(1)}, f32[2048,1,1,64]{0,3,2,1:T(8,128)}, f32[4,512,1,2,64]{1,0,4,3,2:T(4,128)}, s32[4]{0:T(128)S...) while((s32[]{:T(128)}, ...), condition=%wide.region_14.15_spmd.clone, body=%wide.region_12.14_spmd.clone.sunk | while | flops 1377500672 | bytes 126400856 | solution.py:130
  489.1 6.2 dynamic_update_slice.20
  498.4 6.7 fusion.190
  520.5 6.3 dynamic_update_slice.20
  530.5 6.6 fusion.190
  552.4 6.2 dynamic_update_slice.20
  561.8 6.7 fusion.190
  583.8 6.1 dynamic_update_slice.20
  593.1 7.6 fusion.190
  607.2 16.6 %all_to_all.88 = bf16[4,2,32768]{2,1,0:T(2,128)(2,1)} all-to-all(bf16[4,2,32768]{2,1,0:T(2,128)(2,1)S(1)} %reshape.591), channel_id=1, replica_groups=mesh['batch'=2,'seq'=4,'mp'=4] {'seq'}, dimensions={0} | all-to-all | bytes 1048576 | tf_op jit(solution)/shard_map/all_to_all | solution.py:267
  646.4 18.0 %all_to_all.89 = bf16[4,2,32768]{2,1,0:T(2,128)(2,1)} all-to-all(bf16[4,2,32768]{2,1,0:T(2,128)(2,1)S(1)} %reshape.589), channel_id=1, replica_groups=mesh['batch'=2,'seq'=4,'mp'=4] {'seq'}, dimensions={0} | all-to-all | bytes 1048576 | tf_op jit(solution)/shard_map/all_to_all | solution.py:260
  671.8 10.0 convolution_convert_fusion.5
  702.6 35.7 %reduce-scatter.12.cloned.1.call-done = bf16[256,128]{1,0:T(8,128)(2,1)} async-done(((bf16[2048,128]{1,0:T(8,128)(2,1)}), bf16[256,128]{1,0:T(8,128)(2,1)}) %reduce-scatter.12.cloned.1.call-update) | async-done | bytes 65552 | tf_op jit(solution)/shard_map/reduce_scatter | solution.py:310
  739.7 42.9 %reduce-scatter.14.cloned.1.call-done = bf16[512,256]{1,0:T(8,128)(2,1)} async-done(((bf16[512,2048]{1,0:T(8,128)(2,1)}), bf16[512,256]{1,0:T(8,128)(2,1)}) %reduce-scatter.14.cloned.1.call-update) | async-done | bytes 262160 | tf_op jit(solution)/shard_map/reduce_scatter | solution.py:313
  784.5 42.6 %reduce-scatter.8.cloned.1.call-done = bf16[256,512]{1,0:T(8,128)(2,1)} async-done(((bf16[2048,512]{1,0:T(8,128)(2,1)}), bf16[256,512]{1,0:T(8,128)(2,1)}) %reduce-scatter.8.cloned.1.call-update) | async-done | bytes 262160 | tf_op jit(solution)/shard_map/reduce_scatter | solution.py:304
  828.9 156.1 %all-reduce.9.cloned.1.call-done = (bf16[512,2048]{1,0:T(8,128)(2,1)}, bf16[512,2048]{1,0:T(8,128)(2,1)}) async-done(((bf16[512,2048]{1,0:T(8,128)(2,1)}, bf16[512,2048]{1,0:T(8,128)(2,1)}), (bf16[512,2048]{1,0:T(8,128)(2,1)}, bf16[512,2048]{1,0:T(8,128)(2,1)})) %all-reduce.9.cloned.1.call-update) | async-done | bytes 4194320 | tf_op jit(solution)/shard_map/psum | solution.py:203
  988.1 13.7 %all-reduce.2 = (bf16[2048]{0:T(1024)(128)(2,1)S(1)}, bf16[2048]{0:T(1024)(128)(2,1)S(1)}) all-reduce(bf16[2048]{0:T(1024)(128)(2,1)S(1)} %get-tuple-element.211, bf16[2048]{0:T(1024)(128)(2,1)S(1)} %copy-done.35), channel_id=3, replica_groups=mesh['batch'=2,'seq'=4,'mp'=4] {'batch','seq'}, use_global_device_ids=true, to_apply=%region_19.20.clone | all-reduce | flops 4096 | bytes 16384
  1003.2 7.1 fusion.68
  (313 shorter events, 267.0 us)
Async XLA Ops:
  7.2 141.5 %copy-start = (bf16[512,2048]{1,0:T(8,128)(2,1)S(1)}, bf16[512,2048]{1,0:T(8,128)(2,1)}, u32[]{:S(2)}) copy-start(bf16[512,2048]{1,0:T(8,128)(2,1)} %param.22) | copy-start | bytes 6291460
  10.6 9.7 copy-start.4
  10.6 9.7 copy-start.27
  10.6 9.7 copy-start.31
  13.3 8.6 copy-start.17
  13.3 8.6 copy-start.19
  16.4 12.7 %copy-start.33 = (f32[512]{0:T(512)}, f32[512]{0:T(512)S(1)}, u32[]{:S(2)}) copy-start(f32[512]{0:T(512)S(1)} %get-tuple-element.285) | copy-start | bytes 6148
  24.9 13.1 %all-to-all-start.1 = ((bf16[512,4,128]{0,2,1:T(8,128)(2,1)}), bf16[512,4,128]{0,2,1:T(8,128)(2,1)S(1)}, u32[]{:S(2)}, u32[]{:S(2)}) async-start(bf16[512,4,128]{0,2,1:T(8,128)(2,1)} %pad_maximum_fusion.2), calls=%async_computation.1 | async-start | bytes 1048576 | tf_op jit(solution)/shard_map/all_to_all | solution.py:180
  34.2 20.4 %copy-start.24 = (s32[1,2048]{1,0:T(1,128)S(1)}, s32[1,2048]{1,0:T(1,128)}, u32[]{:S(2)}) copy-start(s32[1,2048]{1,0:T(1,128)} %param.17) | copy-start | bytes 24580
  37.9 13.0 %all-to-all-start = ((bf16[512,4,128]{0,2,1:T(8,128)(2,1)}), bf16[512,4,128]{0,2,1:T(8,128)(2,1)}, u32[]{:S(2)}, u32[]{:S(2)}) async-start(bf16[512,4,128]{0,2,1:T(8,128)(2,1)} %fusion.83), calls=%async_computation | async-start | bytes 1048576 | tf_op jit(solution)/shard_map/all_to_all | solution.py:179
  42.1 196.5 %all-reduce.7.cloned.1.call-start = ((), (), s32[]{:S(2)}) async-start(), calls=%async_computation.13 | async-start | bytes 4194304 | tf_op jit(solution)/shard_map/psum | solution.py:194
  103.9 41.4 %copy-start.12 = (bf16[2048,1,2,64]{0,3,2,1:T(8,128)(2,1)}, bf16[2048,1,2,64]{0,3,2,1:T(8,128)(2,1)S(1)}, u32[]{:S(2)}) copy-start(bf16[2048,1,2,64]{0,3,2,1:T(8,128)(2,1)S(1)} %get-tuple-element.534) | copy-start | bytes 1572868
  148.7 93.0 %copy-start.29 = (bf16[512,4,1,128]{0,3,1,2:T(8,128)(2,1)}, bf16[512,4,1,128]{0,3,1,2:T(8,128)(2,1)S(1)}, u32[]{:S(2)}) copy-start(bf16[512,4,1,128]{0,3,1,2:T(8,128)(2,1)S(1)} %copy.94) | copy-start | bytes 1572868
  151.3 90.4 %copy-start.30 = (f32[2048]{0:T(1024)S(1)}, f32[2048]{0:T(1024)}, u32[]{:S(2)}) copy-start(f32[2048]{0:T(1024)} %param.23) | copy-start | bytes 24580
  151.3 283.8 %all-gather.3.cloned.1.call-start = ((), (), s32[]{:S(2)}) async-start(), calls=%async_computation.21 | async-start | bytes 10485760 | tf_op jit(solution)/shard_map/all_gather | solution.py:216
  242.0 8.9 slice-start
  286.3 402.4 %reduce-scatter.16.cloned.1.call-start = ((), (), s32[]{:S(2)}) async-start(), calls=%async_computation.18 | async-start | bytes 9437184 | tf_op jit(solution)/shard_map/reduce_scatter | solution.py:319
  297.1 394.4 %reduce-scatter.18.cloned.1.call-start = ((), (), s32[]{:S(2)}) async-start(), calls=%async_computation.19 | async-start | bytes 9437184 | tf_op jit(solution)/shard_map/reduce_scatter | solution.py:322
  456.1 16.9 %all-to-all-start.3 = ((bf16[512,4,128]{0,2,1:T(8,128)(2,1)}), bf16[512,4,128]{0,2,1:T(8,128)(2,1)S(1)}, u32[]{:S(2)}, u32[]{:S(2)}) async-start(bf16[512,4,128]{0,2,1:T(8,128)(2,1)} %bitcast.386), calls=%async_computation.3 | async-start | bytes 1048576 | tf_op jit(solution)/shard_map/all_to_all | solution.py:241
  459.6 234.7 %reduce-scatter.20.cloned.1.call-start = ((), (), s32[]{:S(2)}) async-start(), calls=%async_computation.20 | async-start | bytes 9437184 | tf_op jit(solution)/shard_map/reduce_scatter | solution.py:325
  470.1 230.9 %reduce-scatter.10.cloned.1.call-start = ((), (), s32[]{:S(2)}) async-start(), calls=%async_computation.15 | async-start | bytes 589824 | tf_op jit(solution)/shard_map/reduce_scatter | solution.py:307
  473.8 128.2 %copy-start.20 = (f32[2048,1,1,32]{0,3,2,1:T(8,128)S(1)}, f32[2048,1,1,32]{0,3,2,1:T(8,128)}, u32[]{:S(2)}) copy-start(f32[2048,1,1,32]{0,3,2,1:T(8,128)} %get-tuple-element.282) | copy-start | bytes 786436
  606.8 21.6 %copy-start.7 = (bf16[512,2048]{1,0:T(8,128)(2,1)S(1)}, bf16[512,2048]{1,0:T(8,128)(2,1)}, u32[]{:S(2)}) copy-start(bf16[512,2048]{1,0:T(8,128)(2,1)} %param.16) | copy-start | bytes 6291460
  606.8 21.6 %copy-start.32 = (f32[2048]{0:T(1024)S(1)}, f32[2048]{0:T(1024)}, u32[]{:S(2)}) copy-start(f32[2048]{0:T(1024)} %param.18) | copy-start | bytes 24580
  606.8 21.6 %copy-start.34 = (f32[512]{0:T(512)S(1)}, f32[512]{0:T(512)}, u32[]{:S(2)}) copy-start(f32[512]{0:T(512)} %copy-done.33) | copy-start | bytes 6148
  630.2 108.0 %reduce-scatter.12.cloned.1.call-start = ((), (), s32[]{:S(2)}) async-start(), calls=%async_computation.16 | async-start | bytes 589824 | tf_op jit(solution)/shard_map/reduce_scatter | solution.py:310
  632.3 150.4 %reduce-scatter.14.cloned.1.call-start = ((), (), s32[]{:S(2)}) async-start(), calls=%async_computation.17 | async-start | bytes 2359296 | tf_op jit(solution)/shard_map/reduce_scatter | solution.py:313
  637.4 189.7 %reduce-scatter.8.cloned.1.call-start = ((), (), s32[]{:S(2)}) async-start(), calls=%async_computation.14 | async-start | bytes 2359296 | tf_op jit(solution)/shard_map/reduce_scatter | solution.py:304
  671.6 10.2 %copy-start.26 = (bf16[2048,128]{1,0:T(8,128)(2,1)S(1)}, bf16[2048,128]{1,0:T(8,128)(2,1)}, u32[]{:S(2)}) copy-start(bf16[2048,128]{1,0:T(8,128)(2,1)} %param.20) | copy-start | bytes 1572868
  671.6 313.4 %all-reduce.9.cloned.1.call-start = ((), (), s32[]{:S(2)}) async-start(), calls=%async_computation.22 | async-start | bytes 8388608 | tf_op jit(solution)/shard_map/psum | solution.py:203
  694.3 293.8 %copy-start.35 = (bf16[2048]{0:T(1024)(128)(2,1)S(1)}, bf16[2048]{0:T(1024)(128)(2,1)}, u32[]{:S(2)}) copy-start(bf16[2048]{0:T(1024)(128)(2,1)} %get-tuple-element.209) | copy-start | bytes 12292
  694.3 308.8 %copy-start.36 = (f32[512]{0:T(512)S(1)}, f32[512]{0:T(512)}, u32[]{:S(2)}) copy-start(f32[512]{0:T(512)} %get-tuple-element.284) | copy-start | bytes 6148
  (34 other events, 150.4 us)
Sparse Core Ops, SparseCore 0:
  151.4 87.0 all-reduce.6
  286.4 148.6 all-gather.2
  438.6 71.0 reduce-scatter.15
  513.0 71.6 reduce-scatter.17
  587.9 78.1 reduce-scatter.19
  669.6 31.3 reduce-scatter.9
  704.1 34.0 reduce-scatter.11
  741.5 41.1 reduce-scatter.13
  786.0 41.0 reduce-scatter.7
  829.9 155.0 all-reduce.8
